TPU v7x, 32 devices: a whole 2x2x4 slice. The times are simulated.
32 devices in a mesh: node: 32 (over z, y, x, core).
Axes of the slice: x: 2, y: 2, z: 4, core: 2. Of those that a mesh axis runs over, the one named last changes fastest.
Arguments:
- round_index: int32 [1], replicated, may hold values from 0 to 63
- sample_ids: int32 [32, 8], P('node'), may hold values from 0 to 3
- token_pool: bfloat16 [32, 4, 64, 512], P('node'), may hold values from -20 to 20
- cotangent_pool: bfloat16 [32, 4, 64, 512], P('node'), may hold values from -6 to 6
- weights: bfloat16 [32, 4, 512, 512], P('node'), may hold values from -12 to 12
- residue: bfloat16 [32, 4, 512, 512], P('node'), may hold values from -6 to 6
Outputs:
- new_weights: bfloat16 [32, 4, 512, 512], P('node')
- new_residue: bfloat16 [32, 4, 512, 512], P('node')
- grad_rms: float32 [], replicated
All inputs are finite; a program needn't handle non-finite values.
Results may differ from a plain program's by a relative error of at most 0.0065.
Values may be sent and summed in bfloat16 or wider, within the bound.
A program may use at most 128 MiB of HBM per device.

v0:
```python
from functools import partial
import math

import jax
import jax.numpy as jnp
from jax import lax
from jax.sharding import PartitionSpec as P

HEAD_DIM = 64


epsilon = 1e-06
step_rate = 0.1


def for_sending(x):

    def short(part):
        return part.astype(jnp.bfloat16) if part.dtype == jnp.float32 else part

    return jax.tree.map(short, x)


def from_behind(block, axis, distance):
    devices = range(lax.axis_size(axis))
    route = [((i - distance) % len(devices), i) for i in devices]
    return lax.ppermute(block, axis, route)


def normalize(tokens):
    values = tokens.astype(jnp.float32)
    centered = values - jnp.mean(values, -1, keepdims=True)
    variance = jnp.mean(centered * centered, -1, keepdims=True)
    return (centered * lax.rsqrt(variance + epsilon)).astype(jnp.bfloat16)


def attend(head_scale, block_data):
    queries, key_rows, value_rows, context_grad = block_data
    scores = (
        jnp.einsum("bshe,bthe->bhst", queries, key_rows, preferred_element_type=jnp.float32)
        * head_scale
    )
    attn_probs = jnp.exp(scores - jnp.max(scores, -1, keepdims=True))
    attn_probs = attn_probs / jnp.sum(attn_probs, -1, keepdims=True)
    probs_half = attn_probs.astype(jnp.bfloat16)
    context = jnp.einsum(
        "bhst,bthe->bshe", probs_half, value_rows, preferred_element_type=jnp.float32
    ).astype(jnp.bfloat16)
    probs_grad = jnp.einsum(
        "bshe,bthe->bhst", context_grad, value_rows, preferred_element_type=jnp.float32
    )
    value_grad = jnp.einsum(
        "bhst,bshe->bthe", probs_half, context_grad, preferred_element_type=jnp.float32
    ).astype(jnp.bfloat16)
    score_grad = (
        attn_probs * (probs_grad - jnp.sum(probs_grad * attn_probs, -1, keepdims=True)) * head_scale
    ).astype(jnp.bfloat16)
    query_grad = jnp.einsum(
        "bhst,bthe->bshe", score_grad, key_rows, preferred_element_type=jnp.float32
    ).astype(jnp.bfloat16)
    key_grad = jnp.einsum(
        "bhst,bshe->bthe", score_grad, queries, preferred_element_type=jnp.float32
    ).astype(jnp.bfloat16)
    return (context, query_grad, key_grad, value_grad)


def local_gradient(weights, tokens, cotangent):
    batch_size, seq_len, model_width = tokens.shape
    head_count = model_width // HEAD_DIM
    proj_scale = model_width ** (-0.5)
    row_count = batch_size * seq_len
    normed_rows = normalize(tokens).reshape(row_count, model_width)
    grad_rows = cotangent.reshape(row_count, model_width)
    projected = (
        jnp.einsum("td,mde->mte", normed_rows, weights[:3], preferred_element_type=jnp.float32)
        * proj_scale
    ).astype(jnp.bfloat16)
    context_grad = (
        jnp.einsum("te,de->td", grad_rows, weights[3], preferred_element_type=jnp.float32)
        * proj_scale
    ).astype(jnp.bfloat16)
    group_size = math.gcd(batch_size, max(1, 512 // seq_len))
    block_shape = (batch_size // group_size, group_size, seq_len, head_count, HEAD_DIM)
    blocks = (
        projected[0].reshape(block_shape),
        projected[1].reshape(block_shape),
        projected[2].reshape(block_shape),
        context_grad.reshape(block_shape),
    )
    context, query_grad, key_grad, value_grad = lax.map(partial(attend, HEAD_DIM ** (-0.5)), blocks)
    stacked = jnp.stack([query_grad, key_grad, value_grad]).reshape(3, row_count, model_width)
    input_grads = (
        jnp.einsum("td,mte->mde", normed_rows, stacked, preferred_element_type=jnp.float32)
        * proj_scale
    )
    output_grad = (
        jnp.einsum(
            "td,te->de",
            context.reshape(row_count, model_width),
            grad_rows,
            preferred_element_type=jnp.float32,
        )
        * proj_scale
    )
    return jnp.concatenate([input_grads, output_grad[None]], 0)


def tracked_from(payload, offset):
    return jax.tree.map(
        lambda part, own: part.astype(own.dtype),
        from_behind(for_sending(payload), "node", offset),
        payload,
    )


def sent_from(payload, offset):
    return jax.tree.map(
        lambda part, own: part.astype(own.dtype),
        from_behind(for_sending(payload), "node", offset),
        payload,
    )


def form_sent(weight_values, tracker):
    return (weight_values.astype(jnp.float32) - step_rate * tracker).astype(jnp.bfloat16)


def per_device(round_index, sample_ids, token_pool, cotangent_pool, weights, residue):
    node_count = lax.axis_size("node")
    levels = node_count.bit_length() - 1
    level_index = round_index[0] % levels
    own_weights = weights[0]
    sample_rows = sample_ids[0]
    tokens = jnp.take(token_pool[0], sample_rows, axis=0)
    cotangent = jnp.take(cotangent_pool[0], sample_rows, axis=0)
    gradient = local_gradient(own_weights, tokens, cotangent)
    total = lax.psum(jnp.sum(gradient * gradient), "node")
    tracked = (residue[0].astype(jnp.float32) + gradient).astype(jnp.bfloat16)
    near_sums = lax.switch(
        level_index,
        [partial(tracked_from, tracked, 2**shift_level) for shift_level in range(levels)],
    )
    tracker = 0.5 * (tracked.astype(jnp.float32) + near_sums.astype(jnp.float32))
    own_sent = form_sent(own_weights, tracker)
    peer_sent = lax.switch(
        level_index, [partial(sent_from, own_sent, 2**shift_level) for shift_level in range(levels)]
    )
    mixed = (
        0.5 * own_weights.astype(jnp.float32)
        + 0.5 * peer_sent.astype(jnp.float32)
        - 0.5 * step_rate * tracker
    )
    new_weights = mixed.astype(jnp.bfloat16)
    new_residue = (tracker - gradient).astype(jnp.bfloat16)
    grad_rms = jnp.sqrt(total / (node_count * gradient.size))
    return (new_weights[None], new_residue[None], grad_rms)


def solution(mesh):
    placed = (
        P(),
        P("node", None),
        P("node", None, None, None),
        P("node", None, None, None),
        P("node", None, None, None),
        P("node", None, None, None),
    )
    return jax.shard_map(
        per_device,
        mesh=mesh,
        in_specs=placed,
        out_specs=(P("node", None, None, None), P("node", None, None, None), P()),
        check_vma=False,
    )
```

profile of v0, /device:TPU:0, one launch (start us, length us, event | category | flops | bytes accessed | tf_op | source)
XLA Modules:
  0.0 192.0 jit_solution(13560851788610266186)
XLA Ops:
  6.0 1.5 fusion.44
  8.8 2.4 %fusion.32 = bf16[3,512,512]{2,1,0:T(8,128)(2,1)S(1)} fusion(bf16[512,512,1]{1,0,2:T(8,128)(2,1)S(1)} %bitcast.75, bf16[1,4,512,512]{3,2,1,0:T(8,128)(2,1)} %param.22), kind=kOutput, calls=%fused_computation.39 | convolution fusion | flops 806879232 | bytes 3670016 | tf_op jit(solution)/shard_map/td,mde->mte/dot_general | solution.py:75
  13.6 1.6 squeeze.39
  15.3 1.5 copy.56
  16.7 1.6 squeeze.35
  18.4 1.5 copy.47
  19.8 3.1 %fusion.66 = f32[8,8,64,64]{2,3,1,0:T(8,128)} fusion(bf16[8,64,8,64]{1,3,2,0:T(8,128)(2,1)S(1)} %copy.50, bf16[8,64,8,64]{1,3,2,0:T(8,128)(2,1)} %copy.56), kind=kOutput, calls=%fused_computation.78 | convolution fusion | flops 33554432 | bytes 2097152 | tf_op jit(solution)/shard_map/while/body/eval_jaxpr/bshe,bthe->bhst/dot_general | solution.py:49
  22.9 4.1 %copy.38 = bf16[1,4,512,512]{2,3,1,0:T(8,128)(2,1)} copy(bf16[1,4,512,512]{3,2,1,0:T(8,128)(2,1)} %param.22) | data formatting | bytes 4194304 | tf_op args[4]
  27.0 4.2 %copy.39 = bf16[1,4,512,512]{2,3,1,0:T(8,128)(2,1)} copy(bf16[1,4,512,512]{3,2,1,0:T(8,128)(2,1)} %param.23) | data formatting | bytes 4194304 | tf_op args[5]
  31.3 2.3 %fusion.65 = (f32[8,8,64]{2,1,0:T(8,128)S(1)}, f32[8,8,64,64]{2,3,1,0:T(8,128)}) fusion(bf16[8,64,8,64]{1,3,2,0:T(8,128)(2,1)S(1)} %copy-done.8, bf16[8,64,8,64]{1,3,2,0:T(8,128)(2,1)S(1)} %copy.44), kind=kOutput, calls=%fused_computation.77 | convolution fusion | flops 34340928 | bytes 2113536 | tf_op jit(solution)/shard_map/while/body/eval_jaxpr/sub | solution.py:43
  33.5 2.3 %fusion.35 = bf16[8,64,8,64]{1,3,2,0:T(8,128)(2,1)S(1)} fusion(bf16[8,64,8,64]{1,3,2,0:T(8,128)(2,1)S(1)} %copy.50, f32[8,8,64,64]{2,3,1,0:T(8,128)} %get-tuple-element.78, f32[8,8,64]{2,1,0:T(8,128)S(1)} %get-tuple-element.77), kind=kOutput, calls=%fused_computation.40 | convolution fusion | flops 34340864 | bytes 2113536 | tf_op jit(solution)/shard_map/while/body/eval_jaxpr/bhst,bshe->bthe/dot_general | solution.py:52
  36.5 1.4 reshape.90
  38.0 5.4 %fusion.37 = bf16[8,64,8,64]{1,3,2,0:T(8,128)(2,1)} fusion(bf16[8,64,8,64]{1,3,2,0:T(8,128)(2,1)S(1)} %copy-done.9, f32[8,8,64,64]{2,3,1,0:T(8,128)} %fusion.66, f32[8,8,64,64]{2,3,1,0:T(8,128)} %get-tuple-element.78, f32[8,8,64]{2,1,0:T(8,128)S(1)} %get-tuple-element.77), kind=kOutput, calls=%fused_computation.42 | convolution fusion | flops 35655744 | bytes 3162112 | tf_op jit(solution)/shard_map/while/body/eval_jaxpr/bhst,bshe->bthe/dot_general | solution.py:61
  43.4 5.3 %fusion.40 = bf16[8,64,8,64]{1,3,2,0:T(8,128)(2,1)} fusion(bf16[8,64,8,64]{1,3,2,0:T(8,128)(2,1)S(1)} %copy.44, f32[8,8,64,64]{2,3,1,0:T(8,128)} %fusion.66, f32[8,8,64,64]{2,3,1,0:T(8,128)} %get-tuple-element.78, f32[8,8,64]{2,1,0:T(8,128)S(1)} %get-tuple-element.77), kind=kOutput, calls=%fused_computation.43 | convolution fusion | flops 35655744 | bytes 3162112 | tf_op jit(solution)/shard_map/while/body/eval_jaxpr/bhst,bthe->bshe/dot_general | solution.py:58
  48.7 2.0 %fusion.36 = bf16[8,64,8,64]{1,3,2,0:T(8,128)(2,1)S(1)} fusion(bf16[8,64,8,64]{1,3,2,0:T(8,128)(2,1)S(1)} %copy-done.7, f32[8,8,64,64]{2,3,1,0:T(8,128)} %get-tuple-element.78, f32[8,8,64]{2,1,0:T(8,128)S(1)} %get-tuple-element.77), kind=kOutput, calls=%fused_computation.41 | convolution fusion | flops 34340864 | bytes 2113536 | tf_op jit(solution)/shard_map/while/body/eval_jaxpr/bhst,bthe->bshe/dot_general | solution.py:46
  53.1 2.0 %copy.78 = bf16[8,64,8,64]{1,0,3,2:T(8,128)(2,1)S(1)} copy(bf16[8,64,8,64]{1,3,2,0:T(8,128)(2,1)} %fusion.40) | data formatting | bytes 1048576 | tf_op jit(solution)/shard_map/stack | solution.py:91
  55.1 1.4 reshape.88
  57.8 2.5 %multiply_bitcast_fusion = f32[3,512,512]{1,2,0:T(8,128)S(1)} fusion(bf16[512,512,1]{1,0,2:T(8,128)(2,1)} %bitcast.76, bf16[1,512,512]{1,2,0:T(8,128)(2,1)} %reshape.90, bf16[1,512,512]{1,2,0:T(8,128)(2,1)S(1)} %reshape.89, bf16[1,512,512]{1,2,0:T(8,128)(2,1)} %reshape.88), kind=kOutput, calls=%fused_computation.16 | convolution fusion | flops 807665664 | bytes 5242880 | tf_op jit(solution)/shard_map/td,mte->mde/dot_general | solution.py:93
  60.3 1.6 copy-done.4
  62.8 2.6 %copy.60 = bf16[4,512,512]{2,1,0:T(8,128)(2,1)} copy(bf16[4,512,512]{1,2,0:T(8,128)(2,1)S(1)} %fusion.6) | data formatting | bytes 4194304 | tf_op jit(solution)/shard_map/convert_element_type | solution.py:138
  65.5 30.4 %conditional.8 = (bf16[4,512,512]{2,1,0:T(8,128)(2,1)}) conditional(s32[]{:T(128)} %clamp.4, bf16[4,512,512]{2,1,0:T(8,128)(2,1)} %copy.60, bf16[4,512,512]{2,1,0:T(8,128)(2,1)} %copy.60, bf16[4,512,512]{2,1,0:T(8,128)(2,1)} %copy.60, bf16[4,512,512]{2,1,0:T(8,128)(2,1)} %copy.60, bf16[4,512,512]{2,1,0:T(8,128)(2,1)} %copy.60), branch_computations={%region_5.7_spmd, %region_6.8_spmd, %region_7.9_spmd, %region_8.10... | conditional | bytes 8388656
  66.0 29.9 %collective-permute-done = bf16[4,512,512]{2,1,0:T(8,128)(2,1)} collective-permute-done((bf16[4,512,512]{2,1,0:T(8,128)(2,1)}, bf16[4,512,512]{2,1,0:T(8,128)(2,1)}, u32[]{:S(2)}, u32[]{:S(2)}) %collective-permute-start) | collective-permute-done | bytes 2097184 | tf_op jit(solution)/shard_map/cond/branch_0_fun/ppermute | solution.py:27
  95.9 4.1 %copy.65 = bf16[4,512,512]{1,2,0:T(8,128)(2,1)} copy(bf16[4,512,512]{2,1,0:T(8,128)(2,1)} %get-tuple-element.79) | data formatting | bytes 4194304 | tf_op jit(solution)/shard_map/conditional.2
  100.0 3.7 %fusion.2 = bf16[4,512,512]{1,2,0:T(8,128)(2,1)S(1)} fusion(bf16[4,512,512]{1,2,0:T(8,128)(2,1)} %copy.65, bf16[4,512,512]{1,2,0:T(8,128)(2,1)} %copy-done.2, bf16[1,4,512,512]{2,3,1,0:T(8,128)(2,1)} %copy.38), kind=kLoop, calls=%fused_computation.6 | loop fusion | flops 7340032 | bytes 8388608 | tf_op jit(solution)/shard_map/convert_element_type | solution.py:125
  103.8 31.8 %conditional.9 = (bf16[4,512,512]{2,1,0:T(8,128)(2,1)}) conditional(s32[]{:T(128)} %clamp.4, bf16[4,512,512]{1,2,0:T(8,128)(2,1)S(1)} %fusion.2, bf16[4,512,512]{1,2,0:T(8,128)(2,1)S(1)} %fusion.2, bf16[4,512,512]{1,2,0:T(8,128)(2,1)S(1)} %fusion.2, bf16[4,512,512]{1,2,0:T(8,128)(2,1)S(1)} %fusion.2, ...), branch_computations={%region_10.12_spmd, %region_11.13_spmd, %region_12.14_spmd, %regio... | conditional | bytes 12582960
  103.8 2.4 %copy.66 = bf16[4,512,512]{2,1,0:T(8,128)(2,1)} copy(bf16[4,512,512]{1,2,0:T(8,128)(2,1)S(1)} %param.7) | data formatting | bytes 4194304 | tf_op jit(solution)/shard_map/convert_element_type
  106.2 29.4 %collective-permute-done.5 = bf16[4,512,512]{2,1,0:T(8,128)(2,1)} collective-permute-done((bf16[4,512,512]{2,1,0:T(8,128)(2,1)}, bf16[4,512,512]{2,1,0:T(8,128)(2,1)}, u32[]{:S(2)}, u32[]{:S(2)}) %collective-permute-start.5) | collective-permute-done | bytes 2097184 | tf_op jit(solution)/shard_map/cond/branch_0_fun/ppermute | solution.py:27
  135.6 4.3 %copy.71 = bf16[4,512,512]{1,2,0:T(8,128)(2,1)} copy(bf16[4,512,512]{2,1,0:T(8,128)(2,1)} %get-tuple-element.80) | data formatting | bytes 4194304 | tf_op jit(solution)/shard_map/conditional.3
  139.9 6.6 %multiply_reduce_fusion = (f32[]{:T(128)}, bf16[1,4,512,512]{2,3,1,0:T(8,128)(2,1)}, bf16[1,4,512,512]{2,3,1,0:T(8,128)(2,1)}) fusion(f32[1,512,512]{1,2,0:T(8,128)S(1)} %copy.59, f32[3,512,512]{1,2,0:T(8,128)} %copy-done.4, bf16[4,512,512]{1,2,0:T(8,128)(2,1)} %copy.65, bf16[4,512,512]{1,2,0:T(8,128)(2,1)S(1)} %copy-done.3, bf16[4,512,512]{1,2,0:T(8,128)(2,1)} %copy.71, ...), kind=kLoop, calls=%fused_computation.13 | loop fusion | flops 16777215 | bytes 16777220 | tf_op jit(solution)/shard_map/reduce_sum | solution.py:137
  146.5 37.0 %psum.7 = f32[]{:T(128)} all-reduce(f32[]{:T(128)} %get-tuple-element.71), channel_id=1, replica_groups=mesh['node'=32] {'node'}, use_global_device_ids=true, to_apply=%region_16.18 | all-reduce | flops 1 | bytes 8 | tf_op jit(solution)/shard_map/psum | solution.py:137
  184.2 4.3 %copy.73 = bf16[1,4,512,512]{3,2,1,0:T(8,128)(2,1)} copy(bf16[1,4,512,512]{2,3,1,0:T(8,128)(2,1)} %get-tuple-element.72) | data formatting | bytes 4194304
  188.5 2.4 %copy.72 = bf16[1,4,512,512]{3,2,1,0:T(8,128)(2,1)} copy(bf16[1,4,512,512]{2,3,1,0:T(8,128)(2,1)S(1)} %copy-done.5) | data formatting | bytes 4194304
  (55 shorter events, 13.9 us)
Async XLA Ops:
  0.6 1.0 copy-start
  0.6 3.8 %copy-start.13 = (bf16[1,4,64,512]{3,2,1,0:T(8,128)(2,1)S(1)}, bf16[1,4,64,512]{3,2,1,0:T(8,128)(2,1)}, u32[]{:S(2)}) copy-start(bf16[1,4,64,512]{3,2,1,0:T(8,128)(2,1)} %param.21) | copy-start | bytes 786436
  4.4 4.4 %copy-start.14 = (bf16[8,64,512]{2,1,0:T(8,128)(2,1)}, bf16[8,64,512]{2,1,0:T(8,128)(2,1)S(1)}, u32[]{:S(2)}) copy-start(bf16[8,64,512]{2,1,0:T(8,128)(2,1)S(1)} %fusion.48) | copy-start | bytes 1572868
  5.1 0.8 copy-start.10
  27.0 4.3 %copy-start.8 = (bf16[8,64,8,64]{1,3,2,0:T(8,128)(2,1)S(1)}, bf16[8,64,8,64]{1,3,2,0:T(8,128)(2,1)}, u32[]{:S(2)}) copy-start(bf16[8,64,8,64]{1,3,2,0:T(8,128)(2,1)} %copy.47) | copy-start | bytes 1572868
  35.8 2.2 %copy-start.9 = (bf16[8,64,8,64]{1,3,2,0:T(8,128)(2,1)S(1)}, bf16[8,64,8,64]{1,3,2,0:T(8,128)(2,1)}, u32[]{:S(2)}) copy-start(bf16[8,64,8,64]{1,3,2,0:T(8,128)(2,1)} %copy.47) | copy-start | bytes 1572868
  43.4 5.3 %copy-start.7 = (bf16[8,64,8,64]{1,3,2,0:T(8,128)(2,1)S(1)}, bf16[8,64,8,64]{1,3,2,0:T(8,128)(2,1)}, u32[]{:S(2)}) copy-start(bf16[8,64,8,64]{1,3,2,0:T(8,128)(2,1)} %copy.56) | copy-start | bytes 1572868
  50.7 1.6 copy-start.11
  53.1 3.4 %copy-start.12 = (bf16[8,64,8,64]{1,3,2,0:T(8,128)(2,1)S(1)}, bf16[8,64,8,64]{1,3,2,0:T(8,128)(2,1)}, u32[]{:S(2)}) copy-start(bf16[8,64,8,64]{1,3,2,0:T(8,128)(2,1)} %fusion.37) | copy-start | bytes 1572868
  57.8 4.2 %copy-start.6 = (bf16[1,4,512,512]{2,3,1,0:T(8,128)(2,1)S(1)}, bf16[1,4,512,512]{2,3,1,0:T(8,128)(2,1)}, u32[]{:S(2)}) copy-start(bf16[1,4,512,512]{2,3,1,0:T(8,128)(2,1)} %copy.39) | copy-start | bytes 6291460
  60.3 1.7 copy-start.4
  62.8 2.7 %copy-start.2 = (bf16[4,512,512]{1,2,0:T(8,128)(2,1)}, bf16[4,512,512]{1,2,0:T(8,128)(2,1)S(1)}, u32[]{:S(2)}) copy-start(bf16[4,512,512]{1,2,0:T(8,128)(2,1)S(1)} %fusion.6) | copy-start | bytes 6291460
  65.5 30.4 %collective-permute-start = (bf16[4,512,512]{2,1,0:T(8,128)(2,1)}, bf16[4,512,512]{2,1,0:T(8,128)(2,1)}, u32[]{:S(2)}, u32[]{:S(2)}) collective-permute-start(bf16[4,512,512]{2,1,0:T(8,128)(2,1)} %param.2), channel_id=1, source_target_pairs={{31,0},{0,1},{1,2},{2,3},{3,4},{4,5},{5,6},{6,7},{7,8},{8,9},{9,10... | collective-permute-start | bytes 6291464 | tf_op jit(solution)/shard_map/cond/branch_0_fun/ppermute | solution.py:27
  106.2 29.4 %collective-permute-start.5 = (bf16[4,512,512]{2,1,0:T(8,128)(2,1)}, bf16[4,512,512]{2,1,0:T(8,128)(2,1)}, u32[]{:S(2)}, u32[]{:S(2)}) collective-permute-start(bf16[4,512,512]{2,1,0:T(8,128)(2,1)} %copy.66), channel_id=1, source_target_pairs={{31,0},{0,1},{1,2},{2,3},{3,4},{4,5},{5,6},{6,7},{7,8},{8,9},{9,10... | collective-permute-start | bytes 6291464 | tf_op jit(solution)/shard_map/cond/branch_0_fun/ppermute | solution.py:27
  135.6 4.3 %copy-start.3 = (bf16[4,512,512]{1,2,0:T(8,128)(2,1)S(1)}, bf16[4,512,512]{1,2,0:T(8,128)(2,1)}, u32[]{:S(2)}) copy-start(bf16[4,512,512]{1,2,0:T(8,128)(2,1)} %copy-done.2) | copy-start | bytes 6291460
  184.2 4.3 %copy-start.5 = (bf16[1,4,512,512]{2,3,1,0:T(8,128)(2,1)S(1)}, bf16[1,4,512,512]{2,3,1,0:T(8,128)(2,1)}, u32[]{:S(2)}) copy-start(bf16[1,4,512,512]{2,3,1,0:T(8,128)(2,1)} %get-tuple-element.73) | copy-start | bytes 6291460
  184.2 6.7 %copy-start.1 = (bf16[1,4,64,512]{3,2,1,0:T(8,128)(2,1)S(1)}, bf16[1,4,64,512]{3,2,1,0:T(8,128)(2,1)}, u32[]{:S(2)}) copy-start(bf16[1,4,64,512]{3,2,1,0:T(8,128)(2,1)} %param.20) | copy-start | bytes 786436
where the time goes:
time: 194 us; the launch traced here: 192 us
  waiting for transfers between devices  59.3 us (31%)
  local copies, waits for them, and re-layouts  51.1 us (26%)
  blocking collectives  37 us (19%)
  matrix products  27.1 us (14%)
  other arithmetic  13.5 us (7%)
  between operations  3.5 us (2%)
    ppermute x2, waiting for transfers between devices, from_behind(): return lax.ppermute(block, axis, route)  59.3 us
    psum x1, blocking collectives, per_device(): total = lax.psum(jnp.sum(gradient * gradient), 'node')  37 us
    unnamed x34, local copies, waits for them, and re-layouts  17.8 us
    squeeze x8, local copies, waits for them, and re-layouts, local_gradient(): lax.map(partial(attend, HEAD_DIM ** (-0.5)), blocks)  8.84 us
    another operation x2, local copies, waits for them, and re-layouts  8.44 us
    another operation x6, local copies, waits for them, and re-layouts, local_gradient(): jnp.stack([query_grad, key_grad, value_grad])  6.85 us
    reduce_sum x1, other arithmetic, per_device(): total = lax.psum(jnp.sum(gradient * gradient), 'node')  6.63 us
    dot_general x1, matrix products, attend(): jnp.einsum('bhst,bshe->bthe', score_grad, queries, preferred_element_type...  5.38 us
  transfers between devices with their start and end apart: 2, of which 2 were waited for; matrix products, arithmetic and copies ran while one was open for 0% of the time, Pallas kernels for 0%

commit v1 on v0

v1 whole, which is shorter than its diff:
```python
from functools import partial

import jax
import jax.numpy as jnp
from jax import lax
from jax.experimental import pallas as pl
from jax.experimental.pallas import tpu as pltpu
from jax.sharding import PartitionSpec as P

HEAD_DIM = 64
LANES = 128
CHUNK_ROWS = 128

epsilon = 1e-06
step_rate = 0.1

f32, bf16 = jnp.float32, jnp.bfloat16
MESH = pl.DeviceIdType.MESH
VMEM = pl.BlockSpec(memory_space=pltpu.VMEM)
SMEM = pl.BlockSpec(memory_space=pltpu.SMEM)
HBM = pl.BlockSpec(memory_space=pl.ANY)


def dot(left, right, left_dim=1, right_dim=0):
    return lax.dot_general(
        left, right, (((left_dim,), (right_dim,)), ((), ())), preferred_element_type=f32
    )


def factors_kernel(ids_ref, tokens_ref, cot_ref, weights_ref, left_ref, right_ref, context_ref):
    pool, seq, width = tokens_ref.shape[1:]
    batch = ids_ref.shape[1]
    rows = pool * seq
    proj_scale = width**-0.5
    head_scale = HEAD_DIM**-0.5
    pairs = width // LANES

    counts = []
    for image in range(pool):
        count = jnp.int32(0)
        for draw in range(batch):
            count = count + (ids_ref[0, draw] == image).astype(jnp.int32)
        counts.append(count.astype(f32))

    values = tokens_ref[0].reshape(rows, width).astype(f32)
    cot = cot_ref[0].reshape(rows, width)
    centered = values - jnp.mean(values, -1, keepdims=True)
    variance = jnp.mean(centered * centered, -1, keepdims=True)
    unit_rows = centered * lax.rsqrt(variance + epsilon)
    normed = unit_rows.astype(bf16)

    weighted = jnp.concatenate(
        [unit_rows[i * seq : (i + 1) * seq] * counts[i] for i in range(pool)], 0
    )
    left_ref[0] = weighted.T.astype(bf16)

    queries, keys, vals = [
        (dot(normed, weights_ref[0, m]) * proj_scale).astype(bf16) for m in range(3)
    ]
    context_grad = (dot(cot, weights_ref[0, 3], 1, 1) * proj_scale).astype(bf16)
    right_ref[3] = cot

    first = lax.broadcasted_iota(jnp.int32, (seq, LANES), 1) < HEAD_DIM
    units = [(i, j) for i in range(pool) for j in range(pairs)]

    def cut(matrix, unit):
        i, j = unit
        return matrix[i * seq : (i + 1) * seq, j * LANES : (j + 1) * LANES]

    def spread(block):
        zero = jnp.zeros_like(block)
        return jnp.concatenate([jnp.where(first, block, zero), jnp.where(first, zero, block)], 0)

    def gather(block):
        return jnp.where(first, block[:seq], block[seq:])

    queries2 = [spread(cut(queries, u)) for u in units]
    grads2 = [spread(cut(context_grad, u)) for u in units]
    keys1 = [cut(keys, u) for u in units]
    vals1 = [cut(vals, u) for u in units]

    scores = [dot(q, k, 1, 1) * head_scale for q, k in zip(queries2, keys1)]
    probs_grad = [dot(g, v, 1, 1) for g, v in zip(grads2, vals1)]
    probs, score_grad = [], []
    for s in scores:
        e = jnp.exp(s - jnp.max(s, -1, keepdims=True))
        probs.append(e / jnp.sum(e, -1, keepdims=True))
    half = [p.astype(bf16) for p in probs]
    for p, g in zip(probs, probs_grad):
        inner = jnp.sum(g * p, -1, keepdims=True)
        score_grad.append((p * (g - inner) * head_scale).astype(bf16))
    for n, (i, j) in enumerate(units):
        at = (slice(i * seq, (i + 1) * seq), slice(j * LANES, (j + 1) * LANES))
        context_ref[at] = gather(dot(half[n], vals1[n])) * counts[i]
        right_ref[2, at[0], at[1]] = dot(half[n], grads2[n], 0, 0).astype(bf16)
        right_ref[0, at[0], at[1]] = gather(dot(score_grad[n], keys1[n])).astype(bf16)
        right_ref[1, at[0], at[1]] = dot(score_grad[n], queries2[n], 0, 0).astype(bf16)
    left_ref[1] = context_ref[...].T.astype(bf16)


def exchange_kernel(
    nodes,
    offset,
    left_ref,
    right_ref,
    weights_ref,
    residue_ref,
    new_weights_ref,
    new_residue_ref,
    total_ref,
    gradient,
    tracked,
    tracked_in,
    sent,
    sent_in,
    weights_out,
    residue_out,
    squares,
    squares_in,
    track_send,
    track_recv,
    sent_send,
    sent_recv,
    out_sems,
    sum_send,
    sum_recv,
):
    me = lax.axis_index("node")
    target = lax.rem(me + offset, nodes)
    source = lax.rem(me + nodes - offset, nodes)
    steps = nodes.bit_length() - 1
    strides = [offset] + [2**k for k in range(steps) if 2**k != offset]
    partners = [me + stride * (1 - 2 * ((me // stride) % 2)) for stride in strides]
    matrices, width = weights_ref.shape[1], weights_ref.shape[2]
    per_matrix = width // CHUNK_ROWS
    chunks = matrices * per_matrix
    proj_scale = width**-0.5

    barrier = pltpu.get_barrier_semaphore()
    for other in [target, source] + partners:
        pl.semaphore_signal(barrier, inc=1, device_id=(other,), device_id_type=MESH)
    pl.semaphore_wait(barrier, 2 + steps)

    def place(c):
        return c // per_matrix, pl.ds((c % per_matrix) * CHUNK_ROWS, CHUNK_ROWS)

    def track_copy(c):
        return pltpu.make_async_remote_copy(
            tracked.at[c], tracked_in.at[c], track_send.at[c], track_recv.at[c], (target,), MESH
        )

    def sent_copy(c):
        return pltpu.make_async_remote_copy(
            sent.at[c], sent_in.at[c], sent_send.at[c], sent_recv.at[c], (target,), MESH
        )

    def residue_copy(c):
        m, rows = place(c)
        return pltpu.make_async_copy(
            residue_out.at[c], new_residue_ref.at[0, m, rows], out_sems.at[0, c]
        )

    def weights_copy(c):
        m, rows = place(c)
        return pltpu.make_async_copy(
            weights_out.at[c], new_weights_ref.at[0, m, rows], out_sems.at[1, c]
        )

    squares[...] = jnp.zeros_like(squares)

    @pl.loop(0, chunks)
    def _(c):
        m, rows = place(c)
        grad = dot(left_ref[m // 3, rows], right_ref[m]) * proj_scale
        gradient[c] = grad
        tracked[c] = (residue_ref[0, m, rows].astype(f32) + grad).astype(bf16)
        track_copy(c).start()
        squares[0] += jnp.sum((grad * grad).reshape(-1, 8, width), 0)

    folded = squares[0]
    squares[0, :, 0:LANES] = sum(
        folded[:, i * LANES : (i + 1) * LANES] for i in range(width // LANES)
    )

    def sum_copy(k):
        return pltpu.make_async_remote_copy(
            squares.at[k, :, pl.ds(0, LANES)],
            squares_in.at[k],
            sum_send.at[k],
            sum_recv.at[k],
            (partners[k],),
            MESH,
        )

    def sum_finish(k):
        sum_copy(k).wait()
        squares[k + 1, :, 0:LANES] = squares[k, :, 0:LANES] + squares_in[k]

    sum_copy(0).start()

    @pl.loop(0, chunks)
    def _(c):
        m, rows = place(c)
        track_copy(c).wait_recv()
        tracker = 0.5 * (tracked[c].astype(f32) + tracked_in[c].astype(f32))
        own = weights_ref[0, m, rows].astype(f32)
        sent[c] = (own - step_rate * tracker).astype(bf16)
        sent_copy(c).start()
        residue_out[c] = (tracker - gradient[c]).astype(bf16)
        residue_copy(c).start()
        gradient[c] = 0.5 * own - 0.5 * step_rate * tracker

    sum_finish(0)
    cuts = [(chunks * k) // steps for k in range(steps + 1)]
    for k in range(steps):
        if k >= 1:
            sum_copy(k).start()

        @pl.loop(cuts[k], cuts[k + 1])
        def _(c):
            sent_copy(c).wait_recv()
            weights_out[c] = (gradient[c] + 0.5 * sent_in[c].astype(f32)).astype(bf16)
            weights_copy(c).start()

        if k >= 1:
            sum_finish(k)
    total_ref[...] = squares[steps, :, 0:LANES]

    @pl.loop(0, chunks)
    def _(c):
        track_copy(c).wait_send()
        sent_copy(c).wait_send()
        residue_copy(c).wait()
        weights_copy(c).wait()


def exchange(nodes, level, left, right, weights, residue):
    matrices, width = weights.shape[1], weights.shape[2]
    chunks = matrices * (width // CHUNK_ROWS)
    steps = nodes.bit_length() - 1
    chunked = (chunks, CHUNK_ROWS, width)
    return pl.pallas_call(
        partial(exchange_kernel, nodes, 2**level),
        out_shape=(
            jax.ShapeDtypeStruct(weights.shape, bf16),
            jax.ShapeDtypeStruct(weights.shape, bf16),
            jax.ShapeDtypeStruct((8, LANES), f32),
        ),
        in_specs=[VMEM] * 4,
        out_specs=(HBM, HBM, VMEM),
        scratch_shapes=[
            pltpu.VMEM(chunked, f32),
            pltpu.VMEM(chunked, bf16),
            pltpu.VMEM(chunked, bf16),
            pltpu.VMEM(chunked, bf16),
            pltpu.VMEM(chunked, bf16),
            pltpu.VMEM(chunked, bf16),
            pltpu.VMEM(chunked, bf16),
            pltpu.VMEM((steps + 1, 8, width), f32),
            pltpu.VMEM((steps, 8, LANES), f32),
            pltpu.SemaphoreType.DMA((chunks,)),
            pltpu.SemaphoreType.DMA((chunks,)),
            pltpu.SemaphoreType.DMA((chunks,)),
            pltpu.SemaphoreType.DMA((chunks,)),
            pltpu.SemaphoreType.DMA((2, chunks)),
            pltpu.SemaphoreType.DMA((steps,)),
            pltpu.SemaphoreType.DMA((steps,)),
        ],
        compiler_params=pltpu.CompilerParams(collective_id=level, has_side_effects=True),
    )(left, right, weights, residue)


def per_device(round_index, sample_ids, token_pool, cotangent_pool, weights, residue):
    nodes = lax.axis_size("node")
    levels = nodes.bit_length() - 1
    pool, seq, width = token_pool.shape[1:]
    rows = pool * seq
    left, right = pl.pallas_call(
        factors_kernel,
        out_shape=(
            jax.ShapeDtypeStruct((2, width, rows), bf16),
            jax.ShapeDtypeStruct((4, rows, width), bf16),
        ),
        in_specs=[SMEM, VMEM, VMEM, VMEM],
        out_specs=(VMEM, VMEM),
        scratch_shapes=[pltpu.VMEM((rows, width), f32)],
    )(sample_ids, token_pool, cotangent_pool, weights)
    new_weights, new_residue, squares = lax.switch(
        round_index[0] % levels,
        [partial(exchange, nodes, level) for level in range(levels)],
        left,
        right,
        weights,
        residue,
    )
    grad_rms = jnp.sqrt(jnp.sum(squares) / (nodes * weights.size))
    return (new_weights, new_residue, grad_rms)


def solution(mesh):
    placed = (
        P(),
        P("node", None),
        P("node", None, None, None),
        P("node", None, None, None),
        P("node", None, None, None),
        P("node", None, None, None),
    )
    return jax.shard_map(
        per_device,
        mesh=mesh,
        in_specs=placed,
        out_specs=(P("node", None, None, None), P("node", None, None, None), P()),
        check_vma=False,
    )
```

time: 194 us -> 116 us (0.60)
  Pallas kernels: 0 us -> 106 us
  waiting for transfers between devices: 59.3 us -> 0 us
  local copies, waits for them, and re-layouts: 51.1 us -> 4.52 us
  blocking collectives: 37 us -> 0 us
  matrix products: 27.1 us -> 0 us
  other arithmetic: 13.5 us -> 1.29 us
    pallas_call x0 -> x2, Pallas kernels: none -> 106 us  [the longest x1 101 us: exchange(): pl.pallas_call(partial(exchange_kernel, nodes, 2 ** level), out_shape=(ja...]
    ppermute x2 -> x0, waiting for transfers between devices: 59.3 us -> none  [from_behind(): return lax.ppermute(block, axis, route)]
    psum x1 -> x0, blocking collectives: 37 us -> none  [per_device(): total = lax.psum(jnp.sum(gradient * gradient), 'node')]
    dot_general x9 -> x0, matrix products: 24.9 us -> none  [the longest x1 5.38 us: attend(): jnp.einsum('bhst,bshe->bthe', score_grad, queries, preferred_element_type...]
    another operation x8 -> x0, local copies, waits for them, and re-layouts: 15.3 us -> none
    unnamed x34 -> x6, local copies, waits for them, and re-layouts: 17.8 us -> 4.52 us
    squeeze x8 -> x0, local copies, waits for them, and re-layouts: 8.84 us -> none  [local_gradient(): lax.map(partial(attend, HEAD_DIM ** (-0.5)), blocks)]
    convert_element_type x3 -> x0, local copies, waits for them, and re-layouts: 5.97 us -> none  [the longest x1 2.65 us: per_device(): tracked = (residue[0].astype(jnp.float32) + gradient).astype(jnp.bfloat16)]
  transfers between devices with their start and end apart: 2 -> 0, of which waited for: 2 -> 0; matrix products, arithmetic and copies ran while one was open for 0% -> 0% of each run, Pallas kernels for 0% -> 0%
where the time goes in v1:
time: 116 us; the launch traced here: 115 us
  Pallas kernels  106 us (91%)
  local copies, waits for them, and re-layouts  4.52 us (4%)
  between operations  2.6 us (2%)
  other arithmetic  1.29 us (1%)
    pallas_call x1, Pallas kernels, exchange(): pl.pallas_call(partial(exchange_kernel, nodes, 2 ** level), out_shape=(ja...  101 us
    pallas_call x1, Pallas kernels, per_device(): pl.pallas_call(factors_kernel, out_shape=(jax.ShapeDtypeStruct((2, width,...  5.05 us
    unnamed x6, local copies, waits for them, and re-layouts  4.52 us

profile of v1, /device:TPU:0, one launch (start us, length us, event | category | flops | bytes accessed | tf_op | source)
XLA Modules:
  0.0 115.5 jit_solution(4399694448561335214)
XLA Ops:
  0.6 0.0 copy-start
  1.5 5.1 %shard_map.95 = (bf16[2,512,256]{2,1,0:T(8,128)(2,1)}, bf16[4,256,512]{2,1,0:T(8,128)(2,1)S(1)}) custom-call(s32[1,8]{1,0:T(1,128)} %ids_ref.1, bf16[1,4,64,512]{3,2,1,0:T(8,128)(2,1)} %tokens_ref.1, bf16[1,4,64,512]{3,2,1,0:T(8,128)(2,1)} %cot_ref.1, bf16[1,4,512,512]{3,2,1,0:T(8,128)(2,1)} %weights_ref.1), custom_call_target="tpu_custom_call" | custom-call | tf_op jit(solution)/shard_map/pallas_call | solution.py:278
  6.5 0.0 copy-done
  6.5 103.3 %conditional.1 = (bf16[1,4,512,512]{3,2,1,0:T(8,128)(2,1)}, bf16[1,4,512,512]{3,2,1,0:T(8,128)(2,1)}, f32[]{:T(128)}) conditional(s32[]{:T(128)} %clamp.3, (bf16[2,512,256]{2,1,0:T(8,128)(2,1)}, bf16[4,256,512]{2,1,0:T(8,128)(2,1)S(1)}, bf16[1,4,512,512]{3,2,1,0:T(8,128)(2,1)S(1)}, ...), branch_computations={%region_0.2_spmd, %region_2.4_spmd, %region_4.6_spmd, %region_6.8_... | conditional | flops 1024 | bytes 4148 | solution.py:288
  6.5 101.3 %branch_3_fun.1 = (bf16[1,4,512,512]{3,2,1,0:T(8,128)(2,1)}, bf16[1,4,512,512]{3,2,1,0:T(8,128)(2,1)}, f32[8,128]{1,0:T(8,128)}) custom-call(bf16[2,512,256]{2,1,0:T(8,128)(2,1)} %get-tuple-element.77.left_ref, bf16[4,256,512]{2,1,0:T(8,128)(2,1)S(1)} %get-tuple-element.78.right_ref, bf16[1,4,512,512]{3,2,1,0:T(8,128)(2,1)S(1)} %get-tuple-element.79.weights_ref, ...), custom_call_target="tpu_custom_call" | custom-call | tf_op jit(solution)/shard_map/cond/branch_3_fun/pallas_call | solution.py:242
  107.8 1.3 %reduce_sum.24 = f32[]{:T(128)} reduce(f32[8,128]{1,0:T(8,128)} %get-tuple-element.83, f32[]{:T(128)} %constant.20.clone), dimensions={0,1}, to_apply=%region_7.7 | reduce | flops 1023 | bytes 4104 | tf_op jit(solution)/shard_map/reduce_sum | solution.py:296
  109.8 0.0 copy-start.1
  109.8 3.2 %copy.37 = bf16[1,4,512,512]{3,2,1,0:T(8,128)(2,1)} copy(bf16[1,4,512,512]{3,2,1,0:T(8,128)(2,1)} %get-tuple-element.127) | data formatting | bytes 4194304
  113.0 0.0 copy-done.1
  113.0 1.3 %copy.38 = bf16[1,4,512,512]{3,2,1,0:T(8,128)(2,1)} copy(bf16[1,4,512,512]{3,2,1,0:T(8,128)(2,1)S(1)} %copy-done.1) | data formatting | bytes 4194304
Async XLA Ops:
  0.6 5.9 %copy-start = (bf16[1,4,512,512]{3,2,1,0:T(8,128)(2,1)S(1)}, bf16[1,4,512,512]{3,2,1,0:T(8,128)(2,1)}, u32[]{:S(2)}) copy-start(bf16[1,4,512,512]{3,2,1,0:T(8,128)(2,1)} %weights_ref.1) | copy-start | bytes 6291460
  109.8 3.2 %copy-start.1 = (bf16[1,4,512,512]{3,2,1,0:T(8,128)(2,1)S(1)}, bf16[1,4,512,512]{3,2,1,0:T(8,128)(2,1)}, u32[]{:S(2)}) copy-start(bf16[1,4,512,512]{3,2,1,0:T(8,128)(2,1)} %get-tuple-element.128) | copy-start | bytes 6291460
